TPU v7x, 32 devices: a whole 2x2x4 slice. The times are simulated.
32 devices in a mesh: ma: 16 (over z, x, core), af: 2 (over y).
Axes of the slice: x: 2, y: 2, z: 4, core: 2. Of those that a mesh axis runs over, the one named last changes fastest.
Arguments:
- coeffs: bfloat16 [512, 128, 2049], P('ma', 'af'), parts along dimension 1, may hold values from -6 to 6
- legendre: bfloat16 [512, 256, 2049], P('ma'), may hold values from -0.1875 to 0.1875
- assign: int32 [512], P('ma'), may hold values from 0 to 511, each once
Outputs:
- fourier: float32 [512, 128, 1024], P('ma', 'af'), parts along dimension 1
There are 2 independent parts, one for each index of `af`. A program takes and returns all parts, laid end to end along the dimension named above; an argument that names none is the same for every part. Nothing has to cross between parts.
Inputs may be any that keep to these rules, and one draw needn't show every extreme that they name: Slot s carries the wavenumbers assign[s] and 2047 - assign[s]; every pair appears once.
All inputs are finite; a program needn't handle non-finite values.
Results may differ from a plain program's by a relative error of at most 0.0003.
Values sent between devices are 32-bit elements; how exact they have to be, the bound alone decides.
No kernel may reach another device: no remote copies, remote signals or barrier semaphores. Data moves between devices by JAX's collectives and lax.ppermute only.
A program may use at most 128 MiB of HBM per device.

v0:
```python
import jax
import jax.numpy as jnp
from jax import lax
from jax.sharding import PartitionSpec as P

TRUNC = 2047


def synthesize(coeffs, legendre, pair_ids):
    slots = coeffs.shape[0]
    columns = coeffs.shape[1]
    width = coeffs.shape[2]
    entry = lax.broadcasted_iota(jnp.int32, (slots, width), 1)
    first_len = (TRUNC + 1 - pair_ids)[:, None]
    second = entry >= first_len
    degree_gap = jnp.where(second, entry - first_len, entry)
    odd_gap = degree_gap % 2 == 1
    zero_value = jnp.zeros((), coeffs.dtype)
    group_masks = jnp.stack(
        [
            jnp.logical_and(jnp.logical_not(second), jnp.logical_not(odd_gap)),
            jnp.logical_and(jnp.logical_not(second), odd_gap),
            jnp.logical_and(second, jnp.logical_not(odd_gap)),
            jnp.logical_and(second, odd_gap),
        ],
        axis=1,
    )
    masked = jnp.where(group_masks[:, :, None, :], coeffs[:, None, :, :], zero_value)
    masked = masked.reshape(slots, 4 * columns, width)
    partial_value = jnp.einsum("shk,sgk->hgs", legendre, masked, preferred_element_type=jnp.float32)
    lat_half = partial_value.shape[0]
    partial_value = partial_value.reshape(lat_half, 4, columns, slots)
    north_rows = jnp.stack(
        [partial_value[:, 0] + partial_value[:, 1], partial_value[:, 2] + partial_value[:, 3]],
        axis=-1,
    )
    south_rows = jnp.stack(
        [partial_value[:, 0] - partial_value[:, 1], partial_value[:, 2] - partial_value[:, 3]],
        axis=-1,
    )
    north_rows = north_rows.reshape(lat_half, columns, 2 * slots)
    south_rows = south_rows.reshape(lat_half, columns, 2 * slots)
    return jnp.concatenate([north_rows, south_rows[::-1]], axis=0)


def column_places(all_pairs, devices, slots, pieces):
    total = devices * 2 * slots
    half_slots = slots // pieces
    column = jnp.arange(total, dtype=jnp.int32)
    piece_index = column // (devices * 2 * half_slots)
    within_piece = column % (devices * 2 * half_slots)
    source_device = within_piece // (2 * half_slots)
    within = within_piece % (2 * half_slots)
    global_slot = source_device * slots + piece_index * half_slots + within // 2
    owner_pair = jnp.take(all_pairs, global_slot)
    return jnp.where(within % 2 == 0, owner_pair, total - 1 - owner_pair)


def shards(coeffs, legendre, assign):
    devices = lax.axis_size("ma")
    slots = coeffs.shape[0]
    all_pairs = lax.all_gather(assign, "ma", axis=0, tiled=True)
    pieces = 1
    full_rows = synthesize(coeffs, legendre, assign)
    received = lax.all_to_all(full_rows, "ma", split_axis=0, concat_axis=2, tiled=True)
    column_place = column_places(all_pairs, devices, slots, pieces)
    total = received.shape[2]
    source_column = (
        jnp.zeros((total,), jnp.int32).at[column_place].set(jnp.arange(total, dtype=jnp.int32))
    )
    return jnp.take(received, source_column, axis=2)


def solution(mesh):
    return jax.shard_map(
        shards,
        mesh=mesh,
        in_specs=(P("ma", "af", None), P("ma", None, None), P("ma")),
        out_specs=P("ma", "af", None),
        check_vma=False,
    )
```

profile of v0, /device:TPU:11, one launch (start us, length us, event | category | flops | bytes accessed | tf_op | source)
XLA Modules:
  0.0 407.0 jit_solution(9538345013267640959)
XLA Ops:
  0.0 0.7 broadcast_subtract_fusion
  0.7 2.4 not_and_fusion.1
  3.1 1.4 pad_add_fusion
  4.5 14.4 %broadcast_select_fusion = bf16[32,4,64,2049]{3,2,1,0:T(8,128)(2,1)} fusion(pred[32,4,2049]{2,1,0:T(4,128)(4,1)S(1)} %pad_add_fusion, bf16[32,64,2049]{2,1,0:T(8,128)(2,1)} %param.3), kind=kLoop, calls=%fused_computation.3 | loop fusion | flops 16785408 | bytes 42225792 | tf_op jit(solution)/shard_map/jit(_where)/select_n | solution.py:28
  18.9 28.2 %fusion = f32[32,256,256]{2,1,0:T(8,128)} fusion(bf16[32,256,2049]{2,1,0:T(8,128)(2,1)} %bitcast.56, bf16[32,256,2049]{1,0,2:T(8,128)(2,1)} %param.4), kind=kOutput, calls=%fused_computation.4 | convolution fusion | flops 8594128896 | bytes 75530240 | tf_op jit(solution)/shard_map/shk,sgk->hgs/dot_general | solution.py:30
  47.1 5.8 %add_bitcast_fusion.1 = (f32[256,64,32,1]{0,1,3,2:T(8,128)S(1)}, f32[256,64,32,1]{0,1,3,2:T(8,128)}, f32[256,64,32,1]{0,1,2,3:T(8,128)S(1)}, f32[256,64,32,1]{0,1,2,3:T(8,128)S(1)}) fusion(f32[256,4,64,32]{0,2,1,3:T(8,128)} %bitcast.59), kind=kLoop, calls=%fused_computation.17 | loop fusion | flops 2097152 | bytes 16777216 | tf_op jit(solution)/shard_map/add | solution.py:34
  53.2 2.3 copy.41
  55.6 7.3 %rev.3 = f32[256,64,64]{0,1,2:T(8,128)} reverse(f32[256,64,64]{0,1,2:T(8,128)} %bitcast.57), dimensions={0} | reverse | bytes 8388608 | tf_op jit(solution)/shard_map/rev | solution.py:43
  62.8 2.1 pad_maximum_fusion.1
  64.9 0.7 copy-done
  65.6 4.5 %pad_maximum_fusion = f32[512,64,64]{0,1,2:T(8,128)} fusion(f32[256,64,64]{0,1,2:T(8,128)S(1)} %copy-done, f32[256,64,64]{0,1,2:T(8,128)S(1)} %bitcast.58), kind=kLoop, calls=%fused_computation.7 | loop fusion | flops 2097152 | bytes 16777216 | tf_op jit(solution)/shard_map/concatenate | solution.py:43
  70.1 16.2 %copy.42 = f32[512,64,64]{1,2,0:T(8,128)} copy(f32[512,64,64]{0,1,2:T(8,128)} %pad_maximum_fusion) | data formatting | bytes 16777216 | tf_op jit(solution)/shard_map/concatenate | solution.py:43
  86.4 18.4 %reshape.569 = f32[16,1,131072]{2,1,0:T(1,128)} reshape(f32[512,64,64]{2,1,0:T(8,128)} %bitcast.53) | data formatting | bytes 16777216
  104.8 6.7 %all-to-all-start = ((f32[16,1,131072]{2,1,0:T(1,128)}), f32[16,1,131072]{2,1,0:T(1,128)}, u32[]{:S(2)}, u32[]{:S(2)}) async-start(f32[16,1,131072]{2,1,0:T(1,128)} %reshape.569), calls=%async_computation | async-start | bytes 16777216 | tf_op jit(solution)/shard_map/all_to_all | solution.py:65
  111.4 0.6 dynamic-slice
  112.8 178.7 %all-reduce = s32[512]{0:T(512)S(1)} all-reduce(s32[512]{0:T(512)S(1)} %dynamic-update-slice), channel_id=1, replica_groups=mesh['ma'=16,'af'=2] {'ma'}, use_global_device_ids=true, to_apply=%add | all-reduce | flops 512 | bytes 4096
  291.6 6.9 %gather_fusion = s32[1024]{0:T(1024)S(1)} fusion(s32[512]{0:T(512)S(1)} %all-reduce, s32[1024]{0:T(1024)S(1)} %broadcast_clamp_fusion), kind=kCustom, calls=%fused_computation | custom fusion | bytes 12288 | tf_op jit(solution)/shard_map/jit(_take)/gather | solution.py:55
  298.6 4.3 %scatter_custom_fusion = s32[1024]{0:T(1024)S(1)} fusion(s32[1024]{0:T(1024)S(1)} %bitcast.62, s32[1024]{0:T(1024)S(1)} %iota.27, s32[]{:T(128)} %constant.100.clone.1), kind=kCustom, calls=%fused_computation.53 | custom fusion | bytes 4100 | tf_op jit(solution)/shard_map/scatter | solution.py:69
  303.4 25.2 %reduce = f32[16,131072]{1,0:T(8,128)} reduce(f32[16,1,131072]{2,1,0:T(1,128)} %all-to-all-done, f32[]{:T(128)} %broadcast.784), dimensions={1}, to_apply=%all_to_all.13.reduce_sub_computation | reduce | bytes 16777220 | tf_op jit(solution)/shard_map/all_to_all | solution.py:65
  328.7 17.4 %reshape.570 = f32[512,64,64]{2,1,0:T(8,128)} reshape(f32[16,131072]{1,0:T(8,128)} %reduce) | data formatting | bytes 16777216
  346.0 17.7 %copy.49 = f32[32,64,16,64]{1,0,3,2:T(8,128)} copy(f32[32,64,16,64]{1,3,0,2:T(8,128)} %bitcast.54) | data formatting | bytes 16777216 | tf_op jit(solution)/shard_map/all_to_all | solution.py:65
  363.7 18.2 %gather_fusion.1 = f32[1024,32,64]{2,1,0:T(8,128)} fusion(f32[32,64,1024]{1,0,2:T(8,128)} %bitcast.55, s32[1024]{0:T(1024)S(1)} %fusion.6), kind=kCustom, calls=%fused_computation.1 | custom fusion | bytes 16781312 | tf_op jit(solution)/shard_map/jit(_take)/gather | solution.py:71
  381.9 12.3 %select_bitcast_fusion = f32[32,64,1024]{1,0,2:T(8,128)} fusion(f32[1024,32,64]{2,1,0:T(8,128)} %gather_fusion.1, pred[1024]{0:T(1024)(128)(4,1)S(1)} %compare_and_fusion), kind=kLoop, calls=%fused_computation.6 | loop fusion | flops 2097152 | bytes 16778240 | tf_op jit(solution)/shard_map/jit(_take)/select_n | solution.py:71
  394.2 12.7 %copy.46 = f32[32,64,1024]{2,1,0:T(8,128)} copy(f32[32,64,1024]{1,0,2:T(8,128)} %select_bitcast_fusion) | data formatting | bytes 16777216 | tf_op jit(solution)/shard_map/jit(_take)/select_n | solution.py:71
  (16 shorter events, 1.1 us)
Async XLA Ops:
  62.8 2.8 copy-start
  104.8 6.7 %copy-start.2 = (u32[32]{0:T(128)S(1)}, u32[32]{0:T(128)}, u32[]{:S(2)}) copy-start(u32[32]{0:T(128)} %constant.119) | copy-start | bytes 388
  104.8 7.8 %copy-start.1 = (s32[32]{0:T(128)S(1)}, s32[32]{0:T(128)}, u32[]{:S(2)}) copy-start(s32[32]{0:T(128)} %param.5) | copy-start | bytes 388
  104.8 198.1 %all-to-all-start = ((f32[16,1,131072]{2,1,0:T(1,128)}), f32[16,1,131072]{2,1,0:T(1,128)}, u32[]{:S(2)}, u32[]{:S(2)}) async-start(f32[16,1,131072]{2,1,0:T(1,128)} %reshape.569), calls=%async_computation | async-start | bytes 16777216 | tf_op jit(solution)/shard_map/all_to_all | solution.py:65
where the time goes:
time: 413 us; the launch traced here: 407 us
  blocking collectives  179 us (43%)
  local copies, waits for them, and re-layouts  123 us (30%)
  other arithmetic  69.3 us (17%)
  matrix products  28.2 us (7%)
  starting transfers between devices  6.65 us (2%)
    unnamed x1, blocking collectives  179 us
    unnamed x11, local copies, waits for them, and re-layouts  37.3 us
    dot_general x1, matrix products, synthesize(): jnp.einsum('shk,sgk->hgs', legendre, masked, preferred_element_type=jnp.f...  28.2 us
    all_to_all x1, other arithmetic, shards(): lax.all_to_all(full_rows, 'ma', split_axis=0, concat_axis=2, tiled=True)  25.2 us
    all_to_all x2, local copies, waits for them, and re-layouts, shards(): lax.all_to_all(full_rows, 'ma', split_axis=0, concat_axis=2, tiled=True)  18.2 us
    gather x1, local copies, waits for them, and re-layouts, shards(): return jnp.take(received, source_column, axis=2)  18.2 us
    concatenate x1, local copies, waits for them, and re-layouts, synthesize(): return jnp.concatenate([north_rows, south_rows[::-1]], axis=0)  16.2 us
    select_n x1, other arithmetic, synthesize(): jnp.where(group_masks[:, :, None, :], coeffs[:, None, :, :], zero_value)  14.4 us
  transfers between devices with their start and end apart: 1, of which 0 were waited for; matrix products, arithmetic and copies ran while one was open for 3% of the time, Pallas kernels for 0%

commit v1 on v0

v1 whole, which is shorter than its diff:
```python
import jax
import jax.numpy as jnp
from jax import lax
from jax.experimental import pallas as pl
from jax.experimental.pallas import tpu as pltpu
from jax.sharding import PartitionSpec as P

TRUNC = 2047
CHUNK = 8
ROWS = 8


def bands_kernel(pair_ref, coeffs_ref, legendre_ref, out_ref, wide_ref, turned_ref, last_ref):
    width, slots, lats = legendre_ref.shape
    main = width - 1
    columns = coeffs_ref.shape[1]
    devices, _, band, _ = out_ref.shape
    half = devices // 2
    block = wide_ref.shape[0]

    def turn(step, carry):
        rows = pl.ds(pl.multiple_of(step * block, block), block)
        wide_ref[...] = legendre_ref[rows].astype(jnp.float32)
        for slot in range(slots):
            turned_ref[slot, rows, :] = wide_ref[:, slot, :].astype(jnp.bfloat16)
        return carry

    lax.fori_loop(0, main // block, turn, 0)
    last_ref[...] = legendre_ref[main].astype(jnp.float32)

    def one_slot(slot, carry):
        pair = pair_ref[slot]
        first_len = TRUNC + 1 - pair
        value = coeffs_ref[slot].astype(jnp.float32)
        entry = lax.broadcasted_iota(jnp.int32, value.shape, 1)
        second = entry >= first_len
        gap = jnp.where(second, entry - first_len, entry)
        signed = jnp.where((gap & 1) == 1, -value, value)
        groups = [
            jnp.where(second, 0.0, value),
            jnp.where(second, value, 0.0),
            jnp.where(second, 0.0, signed),
            jnp.where(second, signed, 0.0),
        ]
        weights = jnp.concatenate(groups, axis=0)
        total = jnp.dot(
            weights[:, :main].astype(jnp.bfloat16), turned_ref[slot], preferred_element_type=jnp.float32
        )
        total = total + weights[:, main:] * last_ref[pl.ds(slot, 1), :]
        total = total.T
        for place in range(half):
            rows = total[place * band : (place + 1) * band]
            out_ref[place, slot] = rows[:, : 2 * columns]
            out_ref[devices - 1 - place, slot] = rows[:, 2 * columns :]
        return carry

    lax.fori_loop(0, slots, one_slot, 0)


def bands(coeffs, turned, pair_ids, chunk, devices):
    columns, width = coeffs.shape[1:]
    lats = turned.shape[2]
    band = 2 * lats // devices
    shape = (devices, CHUNK, band, 2 * columns)
    return pl.pallas_call(
        bands_kernel,
        grid_spec=pltpu.PrefetchScalarGridSpec(
            num_scalar_prefetch=1,
            grid=(1,),
            in_specs=[
                pl.BlockSpec((CHUNK, columns, width), lambda i, s: (chunk, 0, 0)),
                pl.BlockSpec((width, CHUNK, lats), lambda i, s: (0, chunk, 0)),
            ],
            out_specs=pl.BlockSpec(shape, lambda i, s: (0, 0, 0, 0)),
            scratch_shapes=[
                pltpu.VMEM((128, CHUNK, lats), jnp.float32),
                pltpu.VMEM((CHUNK, width - 1, lats), jnp.bfloat16),
                pltpu.VMEM((CHUNK, lats), jnp.float32),
            ],
        ),
        out_shape=jax.ShapeDtypeStruct(shape, jnp.float32),
        compiler_params=pltpu.CompilerParams(vmem_limit_bytes=56 * 1024 * 1024),
        cost_estimate=pl.CostEstimate(
            flops=2 * CHUNK * lats * width * 4 * columns,
            bytes_accessed=2 * CHUNK * width * (lats + columns) + 4 * devices * CHUNK * band * 2 * columns,
            transcendentals=0,
        ),
        name="bands",
    )(pair_ids, coeffs, turned)


def place_kernel(south_ref, low_ref, high_ref, *refs):
    *received, out_ref = refs
    rows, columns, total = out_ref.shape
    half = total // 2
    south = south_ref[0]
    low, high = [], []
    for row in range(rows):
        pieces = [ref[:, :, row, :] for ref in received]
        pieces = [piece.reshape(-1, piece.shape[-1]).T for piece in pieces]
        value = jnp.concatenate(pieces, axis=1)
        low.append(value[:columns])
        high.append(value[columns:])
    for values, order_ref, start in ((low, low_ref, 0), (high, high_ref, half)):
        value = jnp.concatenate(values, axis=0)
        lead = value.astype(jnp.bfloat16)
        rest = (value - lead.astype(jnp.float32)).astype(jnp.bfloat16)
        order = order_ref[...]
        placed = jnp.dot(lead, order, preferred_element_type=jnp.float32)
        placed = placed + jnp.dot(rest, order, preferred_element_type=jnp.float32)
        for row in range(rows):
            target = jnp.where(south == 1, rows - 1 - row, row)
            out_ref[target, :, start : start + half] = placed[row * columns : (row + 1) * columns]


def place(received, pair_ids, south, lats, columns):
    pairs = pair_ids.shape[0]
    column = lax.broadcasted_iota(jnp.int32, (pairs, pairs), 1)
    low = (pair_ids[:, None] == column).astype(jnp.bfloat16)
    high = (pairs - 1 - pair_ids[:, None] == column).astype(jnp.bfloat16)
    steps = lats // ROWS

    def out_map(i, south_ref):
        return (jnp.where(south_ref[0] == 1, steps - 1 - i, i), 0, 0)

    whole = pl.BlockSpec((pairs, pairs), lambda i, s: (0, 0))
    pieces = [
        pl.BlockSpec((piece.shape[0], piece.shape[1], ROWS, piece.shape[3]), lambda i, s: (0, 0, i, 0))
        for piece in received
    ]
    return pl.pallas_call(
        place_kernel,
        grid_spec=pltpu.PrefetchScalarGridSpec(
            num_scalar_prefetch=1,
            grid=(steps,),
            in_specs=[whole, whole] + pieces,
            out_specs=pl.BlockSpec((ROWS, columns, 2 * pairs), out_map),
        ),
        out_shape=jax.ShapeDtypeStruct((lats, columns, 2 * pairs), jnp.float32),
        compiler_params=pltpu.CompilerParams(vmem_limit_bytes=48 * 1024 * 1024),
        name="place",
    )(south, low, high, *received)


def shards(coeffs, legendre, assign):
    devices = lax.axis_size("ma")
    me = lax.axis_index("ma")
    slots, columns, _ = coeffs.shape
    lats = 2 * legendre.shape[1] // devices
    all_pairs = lax.all_to_all(
        jnp.broadcast_to(assign[None, None, :], (devices, 1, slots)), "ma", 0, 0, tiled=True
    ).reshape(devices, slots)
    turned = jnp.transpose(legendre, (2, 0, 1))
    received, order = [], []
    for start in range(0, slots, CHUNK):
        stop = start + CHUNK
        sent = bands(coeffs, turned, assign[start:stop], start // CHUNK, devices)
        piece = lax.all_to_all(sent.reshape(devices, CHUNK * lats, 2 * columns), "ma", 0, 0, tiled=True)
        received.append(piece.reshape(devices, CHUNK, lats, 2 * columns))
        order.append(all_pairs[:, start:stop].reshape(-1))
    south = (me >= devices // 2).astype(jnp.int32).reshape(1)
    return place(received, jnp.concatenate(order), south, lats, columns)


def solution(mesh):
    return jax.shard_map(
        shards,
        mesh=mesh,
        in_specs=(P("ma", "af", None), P("ma", None, None), P("ma")),
        out_specs=P("ma", "af", None),
        check_vma=False,
    )
```

time: 413 us -> 265 us (0.64); the launches traced: 407 us -> 265 us
  blocking collectives: 179 us -> 0 us
  Pallas kernels: 0 us -> 139 us
  local copies, waits for them, and re-layouts: 123 us -> 4.54 us
  waiting for transfers between devices: 0.01 us -> 93.5 us
  other arithmetic: 69.3 us -> 0.25 us
  matrix products: 28.2 us -> 0 us
  starting transfers between devices: 6.65 us -> 26.9 us
    unnamed x1 -> x0, blocking collectives: 179 us -> none
    pallas_call x0 -> x5, Pallas kernels: none -> 139 us  [the longest x4 128 us: bands(): pl.pallas_call(bands_kernel, grid_spec=pltpu.PrefetchScalarGridSpec(num_s...]
    all_to_all x1 -> x5, waiting for transfers between devices: 0.01 us -> 93.5 us  [the longest x4 93.5 us: shards(): lax.all_to_all(sent.reshape(devices, CHUNK * lats, 2 * columns), 'ma', 0,...]
    unnamed x11 -> x5, local copies, waits for them, and re-layouts: 37.3 us -> 1.38 us
    dot_general x1 -> x0, matrix products: 28.2 us -> none  [synthesize(): jnp.einsum('shk,sgk->hgs', legendre, masked, preferred_element_type=jnp.f...]
    select_n x4 -> x0, other arithmetic: 26.8 us -> none  [the longest x1 14.4 us: synthesize(): jnp.where(group_masks[:, :, None, :], coeffs[:, None, :, :], zero_value)]
    all_to_all x1 -> x0, other arithmetic: 25.2 us -> none  [shards(): lax.all_to_all(full_rows, 'ma', split_axis=0, concat_axis=2, tiled=True)]
    gather x2 -> x0, local copies, waits for them, and re-layouts: 25 us -> none  [the longest x1 18.2 us: shards(): return jnp.take(received, source_column, axis=2)]
  transfers between devices with their start and end apart: 1 -> 5, of which waited for: 0 -> 4; matrix products, arithmetic and copies ran while one was open for 3% -> 1% of each run, Pallas kernels for 0% -> 48%
where the time goes in v1:
time: 265 us
  Pallas kernels  139 us (52%)
  waiting for transfers between devices  93.5 us (35%)
  starting transfers between devices  26.9 us (10%)
  local copies, waits for them, and re-layouts  4.54 us (2%)
    pallas_call x4, Pallas kernels, bands(): pl.pallas_call(bands_kernel, grid_spec=pltpu.PrefetchScalarGridSpec(num_s...  128 us
    all_to_all x4, waiting for transfers between devices, shards(): lax.all_to_all(sent.reshape(devices, CHUNK * lats, 2 * columns), 'ma', 0,...  93.5 us
    all_to_all x4, starting transfers between devices, shards(): lax.all_to_all(sent.reshape(devices, CHUNK * lats, 2 * columns), 'ma', 0,...  20.4 us
    pallas_call x1, Pallas kernels, place(): pl.pallas_call(place_kernel, grid_spec=pltpu.PrefetchScalarGridSpec(num_s...  11.9 us
    all_to_all x1, starting transfers between devices, shards(): lax.all_to_all(jnp.broadcast_to(assign[None, None, :], (devices, 1, slots...  6.52 us
  transfers between devices with their start and end apart: 5, of which 4 were waited for; matrix products, arithmetic and copies ran while one was open for 1% of the time, Pallas kernels for 48%

profile of v1, /device:TPU:11, one launch (start us, length us, event | category | flops | bytes accessed | tf_op | source)
XLA Modules:
  0.0 264.6 jit_solution(511243729755760299)
XLA Ops:
  0.0 1.3 broadcast_in_dim.2
  1.3 6.5 %all-to-all-start = ((s32[16,1,32]{2,1,0:T(1,128)}), s32[16,1,32]{2,1,0:T(1,128)S(1)}, u32[]{:S(2)}, u32[]{:S(2)}) async-start(s32[16,1,32]{2,1,0:T(1,128)} %broadcast_in_dim.2), calls=%async_computation | async-start | bytes 16384 | tf_op jit(solution)/shard_map/all_to_all | solution.py:150
  7.8 1.5 fusion.3
  9.2 31.9 %bands.7 = f32[16,8,32,128]{3,2,1,0:T(8,128)} custom-call(s32[8]{0:T(128)} %get-tuple-element.9.pair_ref, bf16[32,64,2049]{2,1,0:T(8,128)(2,1)} %coeffs_ref.7, bf16[2049,32,256]{2,1,0:T(8,128)(2,1)} %bitcast.12), custom_call_target="tpu_custom_call" | custom-call | flops 2148532224 | bytes 12588032 | tf_op jit(solution)/shard_map/bands/pallas_call | solution.py:65
  41.1 0.0 all-to-all-done
  41.1 6.0 %all-to-all-start.4 = ((f32[16,256,128]{2,1,0:T(8,128)}), f32[16,256,128]{2,1,0:T(8,128)S(1)}, u32[]{:S(2)}, u32[]{:S(2)}) async-start(f32[16,256,128]{2,1,0:T(8,128)} %bitcast.19), calls=%async_computation.4 | async-start | bytes 4194304 | tf_op jit(solution)/shard_map/all_to_all | solution.py:158
  47.1 31.9 %bands.5 = f32[16,8,32,128]{3,2,1,0:T(8,128)} custom-call(s32[8]{0:T(128)} %get-tuple-element.10.pair_ref, bf16[32,64,2049]{2,1,0:T(8,128)(2,1)} %coeffs_ref.7, bf16[2049,32,256]{2,1,0:T(8,128)(2,1)} %bitcast.13), custom_call_target="tpu_custom_call" | custom-call | flops 2148532224 | bytes 12588032 | tf_op jit(solution)/shard_map/bands/pallas_call | solution.py:65
  79.0 15.5 %all-to-all-done.4 = f32[16,256,128]{2,1,0:T(8,128)S(1)} async-done(((f32[16,256,128]{2,1,0:T(8,128)}), f32[16,256,128]{2,1,0:T(8,128)S(1)}, u32[]{:S(2)}, u32[]{:S(2)}) %all-to-all-start.4) | async-done | bytes 2097184 | tf_op jit(solution)/shard_map/all_to_all | solution.py:158
  94.6 1.3 copy-done
  95.9 4.8 %all-to-all-start.2 = ((f32[16,256,128]{2,1,0:T(8,128)}), f32[16,256,128]{2,1,0:T(8,128)S(1)}, u32[]{:S(2)}, u32[]{:S(2)}) async-start(f32[16,256,128]{2,1,0:T(8,128)} %bitcast.20), calls=%async_computation.2 | async-start | bytes 4194304 | tf_op jit(solution)/shard_map/all_to_all | solution.py:158
  100.7 31.9 %bands.4 = f32[16,8,32,128]{3,2,1,0:T(8,128)} custom-call(s32[8]{0:T(128)} %get-tuple-element.11.pair_ref, bf16[32,64,2049]{2,1,0:T(8,128)(2,1)} %coeffs_ref.7, bf16[2049,32,256]{2,1,0:T(8,128)(2,1)} %bitcast.14), custom_call_target="tpu_custom_call" | custom-call | flops 2148532224 | bytes 12588032 | tf_op jit(solution)/shard_map/bands/pallas_call | solution.py:65
  132.5 15.5 %all-to-all-done.2 = f32[16,256,128]{2,1,0:T(8,128)S(1)} async-done(((f32[16,256,128]{2,1,0:T(8,128)}), f32[16,256,128]{2,1,0:T(8,128)S(1)}, u32[]{:S(2)}, u32[]{:S(2)}) %all-to-all-start.2) | async-done | bytes 2097184 | tf_op jit(solution)/shard_map/all_to_all | solution.py:158
  148.1 4.8 %all-to-all-start.1 = ((f32[16,256,128]{2,1,0:T(8,128)}), f32[16,256,128]{2,1,0:T(8,128)}, u32[]{:S(2)}, u32[]{:S(2)}) async-start(f32[16,256,128]{2,1,0:T(8,128)} %bitcast.18), calls=%async_computation.1 | async-start | bytes 4194304 | tf_op jit(solution)/shard_map/all_to_all | solution.py:158
  152.9 31.9 %bands.6 = f32[16,8,32,128]{3,2,1,0:T(8,128)} custom-call(s32[8]{0:T(128)} %get-tuple-element.12.pair_ref, bf16[32,64,2049]{2,1,0:T(8,128)(2,1)} %coeffs_ref.7, bf16[2049,32,256]{2,1,0:T(8,128)(2,1)} %bitcast.15), custom_call_target="tpu_custom_call" | custom-call | flops 2148532224 | bytes 12588032 | tf_op jit(solution)/shard_map/bands/pallas_call | solution.py:65
  184.8 15.6 %all-to-all-done.1 = f32[16,256,128]{2,1,0:T(8,128)} async-done(((f32[16,256,128]{2,1,0:T(8,128)}), f32[16,256,128]{2,1,0:T(8,128)}, u32[]{:S(2)}, u32[]{:S(2)}) %all-to-all-start.1) | async-done | bytes 2097184 | tf_op jit(solution)/shard_map/all_to_all | solution.py:158
  200.4 4.8 %all-to-all-start.3 = ((f32[16,256,128]{2,1,0:T(8,128)}), f32[16,256,128]{2,1,0:T(8,128)}, u32[]{:S(2)}, u32[]{:S(2)}) async-start(f32[16,256,128]{2,1,0:T(8,128)} %bitcast.17), calls=%async_computation.3 | async-start | bytes 4194304 | tf_op jit(solution)/shard_map/all_to_all | solution.py:158
  205.2 0.1 fusion.2
  205.2 0.1 reshape.88
  205.3 0.1 reshape.87
  205.4 0.1 reshape.86
  205.5 0.1 reshape.85
  205.7 0.2 fusion
  205.9 46.7 %all-to-all-done.3 = f32[16,256,128]{2,1,0:T(8,128)} async-done(((f32[16,256,128]{2,1,0:T(8,128)}), f32[16,256,128]{2,1,0:T(8,128)}, u32[]{:S(2)}, u32[]{:S(2)}) %all-to-all-start.3) | async-done | bytes 2097184 | tf_op jit(solution)/shard_map/all_to_all | solution.py:158
  252.7 11.9 %place.1 = f32[32,64,1024]{2,1,0:T(8,128)} custom-call(s32[1]{0:T(128)} %bitcast.south_ref, bf16[512,512]{1,0:T(8,128)(2,1)S(1)} %get-tuple-element.13.low_ref, bf16[512,512]{1,0:T(8,128)(2,1)S(1)} %get-tuple-element.14.high_ref, f32[16,8,32,128]{3,2,1,0:T(8,128)} %bitcast.4.refs_0_, f32[16,8,32,128]{3,2,1,0:T(8,128)S(1)} %bitcast.11, ...), custom_call_target="tpu_custom_call" | custom-call | tf_op jit(solution)/shard_map/place/pallas_call | solution.py:131
  (7 shorter events, 0.1 us)
Async XLA Ops:
  1.3 39.9 %all-to-all-start = ((s32[16,1,32]{2,1,0:T(1,128)}), s32[16,1,32]{2,1,0:T(1,128)S(1)}, u32[]{:S(2)}, u32[]{:S(2)}) async-start(s32[16,1,32]{2,1,0:T(1,128)} %broadcast_in_dim.2), calls=%async_computation | async-start | bytes 16384 | tf_op jit(solution)/shard_map/all_to_all | solution.py:150
  41.1 53.4 %all-to-all-start.4 = ((f32[16,256,128]{2,1,0:T(8,128)}), f32[16,256,128]{2,1,0:T(8,128)S(1)}, u32[]{:S(2)}, u32[]{:S(2)}) async-start(f32[16,256,128]{2,1,0:T(8,128)} %bitcast.19), calls=%async_computation.4 | async-start | bytes 4194304 | tf_op jit(solution)/shard_map/all_to_all | solution.py:158
  94.6 1.3 copy-start
  95.9 52.2 %all-to-all-start.2 = ((f32[16,256,128]{2,1,0:T(8,128)}), f32[16,256,128]{2,1,0:T(8,128)S(1)}, u32[]{:S(2)}, u32[]{:S(2)}) async-start(f32[16,256,128]{2,1,0:T(8,128)} %bitcast.20), calls=%async_computation.2 | async-start | bytes 4194304 | tf_op jit(solution)/shard_map/all_to_all | solution.py:158
  148.1 52.3 %all-to-all-start.1 = ((f32[16,256,128]{2,1,0:T(8,128)}), f32[16,256,128]{2,1,0:T(8,128)}, u32[]{:S(2)}, u32[]{:S(2)}) async-start(f32[16,256,128]{2,1,0:T(8,128)} %bitcast.18), calls=%async_computation.1 | async-start | bytes 4194304 | tf_op jit(solution)/shard_map/all_to_all | solution.py:158
  200.4 52.3 %all-to-all-start.3 = ((f32[16,256,128]{2,1,0:T(8,128)}), f32[16,256,128]{2,1,0:T(8,128)}, u32[]{:S(2)}, u32[]{:S(2)}) async-start(f32[16,256,128]{2,1,0:T(8,128)} %bitcast.17), calls=%async_computation.3 | async-start | bytes 4194304 | tf_op jit(solution)/shard_map/all_to_all | solution.py:158

commit v2 on v1

v2 whole, which is shorter than its diff:
```python
import functools

import jax
import jax.numpy as jnp
from jax import lax
from jax.experimental import pallas as pl
from jax.experimental.pallas import tpu as pltpu
from jax.sharding import PartitionSpec as P

TRUNC = 2047
TILE = 8


def bands_kernel(chunk, extra, pair_ref, coeffs_ref, legendre_ref, *refs):
    if extra:
        pairs_ref, out_ref, wide_ref, turned_ref, last_ref = refs
    else:
        out_ref, wide_ref, turned_ref, last_ref = refs
    width, slots, lats = legendre_ref.shape
    main = width - 1
    columns = coeffs_ref.shape[1]
    devices = out_ref.shape[0]
    half = devices // 2
    band = lats // half
    parts = wide_ref.shape[0]
    block = wide_ref.shape[1] // slots
    first_slot = (chunk + pl.program_id(0)) * slots

    def turn(step, carry):
        rows = pl.ds(pl.multiple_of(step * block, block), block)
        wide = legendre_ref[rows].astype(jnp.float32).reshape(block * slots, lats)
        for part in range(parts):
            wide_ref[part] = wide[:, part * 128 : (part + 1) * 128]
        for slot in range(slots):
            value = jnp.concatenate(
                [
                    wide_ref[part, pl.ds(slot, block, stride=slots), :]
                    for part in range(parts)
                ],
                axis=1,
            )
            turned_ref[slot, rows, :] = value.astype(jnp.bfloat16)
        return carry

    lax.fori_loop(0, main // block, turn, 0)
    last_ref[...] = legendre_ref[main].astype(jnp.float32)

    def one_slot(slot, carry):
        first_len = TRUNC + 1 - pair_ref[first_slot + slot]
        value = coeffs_ref[slot].astype(jnp.float32)
        entry = lax.broadcasted_iota(jnp.int32, value.shape, 1)
        second = entry >= first_len
        gap = jnp.where(second, entry - first_len, entry)
        signed = jnp.where((gap & 1) == 1, -value, value)
        groups = [
            jnp.where(second, 0.0, value),
            jnp.where(second, value, 0.0),
            jnp.where(second, 0.0, signed),
            jnp.where(second, signed, 0.0),
        ]
        weights = jnp.concatenate(groups, axis=0)
        total = jnp.dot(
            weights[:, :main].astype(jnp.bfloat16), turned_ref[slot], preferred_element_type=jnp.float32
        )
        total = total + weights[:, main:] * last_ref[pl.ds(slot, 1), :]
        total = total.T
        for place in range(half):
            for group in range(band // TILE):
                start = place * band + group * TILE
                rows = total[start : start + TILE]
                for owner, part in (
                    (place, rows[:, : 2 * columns]),
                    (devices - 1 - place, rows[:, 2 * columns :]),
                ):
                    if extra:
                        at = pl.multiple_of((group * slots + slot) * TILE, TILE)
                        out_ref[owner, pl.ds(at, TILE), :] = part
                    else:
                        at = pl.multiple_of(slot * TILE, TILE)
                        out_ref[owner, group, pl.ds(at, TILE), :] = part
        return carry

    lax.fori_loop(0, slots, one_slot, 0)
    if extra:
        pairs = pairs_ref[...].astype(jnp.float32)
        row = out_ref.shape[1] - TILE
        for owner in range(devices):
            out_ref[owner, row : row + 1, : pairs.shape[1]] = pairs


def bands(coeffs, turned, assign, chunk, steps, devices):
    columns, width = coeffs.shape[1:]
    lats = turned.shape[2]
    groups = 2 * lats // devices // TILE
    extra = chunk == 0
    in_specs = [
        pl.BlockSpec((TILE, columns, width), lambda i, s: (chunk + i, 0, 0)),
        pl.BlockSpec((width, TILE, lats), lambda i, s: (0, chunk + i, 0)),
    ]
    operands = [assign, coeffs, turned]
    if extra:
        shape = (devices, (groups * TILE + 1) * TILE, 2 * columns)
        out_specs = pl.BlockSpec(shape, lambda i, s: (0, 0, 0))
        in_specs.append(pl.BlockSpec((1, assign.shape[0]), lambda i, s: (0, 0)))
        operands.append(assign.reshape(1, -1))
    else:
        shape = (devices, groups, steps * TILE * TILE, 2 * columns)
        out_specs = pl.BlockSpec((devices, groups, TILE * TILE, 2 * columns), lambda i, s: (0, 0, i, 0))
    return pl.pallas_call(
        functools.partial(bands_kernel, chunk, extra),
        grid_spec=pltpu.PrefetchScalarGridSpec(
            num_scalar_prefetch=1,
            grid=(steps,),
            in_specs=in_specs,
            out_specs=out_specs,
            scratch_shapes=[
                pltpu.VMEM((lats // 128, 128 * TILE, 128), jnp.float32),
                pltpu.VMEM((TILE, width - 1, lats), jnp.bfloat16),
                pltpu.VMEM((TILE, lats), jnp.float32),
            ],
        ),
        out_shape=jax.ShapeDtypeStruct(shape, jnp.float32),
        compiler_params=pltpu.CompilerParams(vmem_limit_bytes=56 * 1024 * 1024),
        cost_estimate=pl.CostEstimate(
            flops=2 * steps * TILE * lats * width * 4 * columns,
            bytes_accessed=2 * steps * TILE * width * (lats + columns),
            transcendentals=0,
        ),
        name="bands",
    )(*operands)


def place_kernel(south_ref, low_ref, high_ref, *refs):
    *received, out_ref = refs
    rows, columns, total = out_ref.shape
    half = total // 2
    south = south_ref[0]
    low, high = [], []
    for row in range(rows):
        pieces = []
        for ref in received:
            slots = ref.shape[-2] // rows
            for source in range(ref.shape[0]):
                picked = pl.ds(row, slots, stride=rows)
                pieces.append(ref[source, picked, :] if len(ref.shape) == 3 else ref[source, 0, picked, :])
        value = jnp.concatenate(pieces, axis=0).T
        low.append(value[:columns])
        high.append(value[columns:])
    for values, order_ref, start in ((low, low_ref, 0), (high, high_ref, half)):
        value = jnp.concatenate(values, axis=0)
        lead = value.astype(jnp.bfloat16)
        rest = (value - lead.astype(jnp.float32)).astype(jnp.bfloat16)
        order = order_ref[...]
        placed = jnp.dot(lead, order, preferred_element_type=jnp.float32)
        placed = placed + jnp.dot(rest, order, preferred_element_type=jnp.float32)
        for row in range(rows):
            target = jnp.where(south == 1, rows - 1 - row, row)
            out_ref[target, :, start : start + half] = placed[row * columns : (row + 1) * columns]


def place(received, pair_ids, south, lats, columns):
    pairs = pair_ids.shape[0]
    column = lax.broadcasted_iota(jnp.int32, (pairs, pairs), 1)
    low = (pair_ids[:, None] == column).astype(jnp.bfloat16)
    high = (pairs - 1 - pair_ids[:, None] == column).astype(jnp.bfloat16)
    steps = lats // TILE

    def out_map(i, south_ref):
        return (jnp.where(south_ref[0] == 1, steps - 1 - i, i), 0, 0)

    whole = pl.BlockSpec((pairs, pairs), lambda i, s: (0, 0))
    pieces = [
        pl.BlockSpec((piece.shape[0], TILE * TILE, piece.shape[2]), lambda i, s: (0, i, 0))
        if len(piece.shape) == 3
        else pl.BlockSpec((piece.shape[0], 1) + piece.shape[2:], lambda i, s: (0, i, 0, 0))
        for piece in received
    ]
    return pl.pallas_call(
        place_kernel,
        grid_spec=pltpu.PrefetchScalarGridSpec(
            num_scalar_prefetch=1,
            grid=(steps,),
            in_specs=[whole, whole] + pieces,
            out_specs=pl.BlockSpec((TILE, columns, 2 * pairs), out_map),
        ),
        out_shape=jax.ShapeDtypeStruct((lats, columns, 2 * pairs), jnp.float32),
        compiler_params=pltpu.CompilerParams(vmem_limit_bytes=48 * 1024 * 1024),
        name="place",
    )(south, low, high, *received)


def shards(coeffs, legendre, assign):
    devices = lax.axis_size("ma")
    me = lax.axis_index("ma")
    slots, columns, _ = coeffs.shape
    lats = 2 * legendre.shape[1] // devices
    turned = jnp.transpose(legendre, (2, 0, 1))
    tiles = slots // TILE
    received = []
    for chunk, steps in ((0, 1), (1, tiles - 1)):
        if steps:
            sent = bands(coeffs, turned, assign, chunk, steps, devices)
            flat = sent.reshape(devices, -1, 2 * columns)
            piece = lax.all_to_all(flat, "ma", 0, 0, tiled=True)
            received.append(piece.reshape(sent.shape))
    all_pairs = received[0][:, TILE * lats, :slots].astype(jnp.int32)
    order = [all_pairs[:, :TILE].reshape(-1), all_pairs[:, TILE:].reshape(-1)]
    south = (me >= devices // 2).astype(jnp.int32).reshape(1)
    return place(received, jnp.concatenate(order), south, lats, columns)


def solution(mesh):
    return jax.shard_map(
        shards,
        mesh=mesh,
        in_specs=(P("ma", "af", None), P("ma", None, None), P("ma")),
        out_specs=P("ma", "af", None),
        check_vma=False,
    )
```

time: 265 us -> 222 us (0.84)
  Pallas kernels: 139 us -> 55 us
  waiting for transfers between devices: 93.5 us -> 155 us
  starting transfers between devices: 26.9 us -> 11.3 us
  local copies, waits for them, and re-layouts: 4.54 us -> 0.28 us
    pallas_call x4 -> x2, Pallas kernels: 128 us -> 44.7 us  [bands(): pl.pallas_call(functools.partial(bands_kernel, chunk, extra), grid_spec=p...]
    all_to_all x5 -> x2, waiting for transfers between devices: 93.5 us -> 155 us  [shards(): piece = lax.all_to_all(flat, 'ma', 0, 0, tiled=True)]
    all_to_all x5 -> x2, starting transfers between devices: 26.9 us -> 11.3 us  [shards(): piece = lax.all_to_all(flat, 'ma', 0, 0, tiled=True)]
  transfers between devices with their start and end apart: 5 -> 2, of which waited for: 4 -> 2; matrix products, arithmetic and copies ran while one was open for 1% -> 0% of each run, Pallas kernels for 48% -> 14%
where the time goes in v2:
time: 222 us
  waiting for transfers between devices  155 us (70%)
  Pallas kernels  55 us (25%)
  starting transfers between devices  11.3 us (5%)
    all_to_all x2, waiting for transfers between devices, shards(): piece = lax.all_to_all(flat, 'ma', 0, 0, tiled=True)  155 us
    pallas_call x2, Pallas kernels, bands(): pl.pallas_call(functools.partial(bands_kernel, chunk, extra), grid_spec=p...  44.7 us
    all_to_all x2, starting transfers between devices, shards(): piece = lax.all_to_all(flat, 'ma', 0, 0, tiled=True)  11.3 us
    pallas_call x1, Pallas kernels, place(): pl.pallas_call(place_kernel, grid_spec=pltpu.PrefetchScalarGridSpec(num_s...  10.3 us
  transfers between devices with their start and end apart: 2, of which 2 were waited for; matrix products, arithmetic and copies ran while one was open for 0% of the time, Pallas kernels for 14%

profile of v2, /device:TPU:11, one launch (start us, length us, event | category | flops | bytes accessed | tf_op | source)
XLA Modules:
  0.0 222.0 jit_solution(16667841263487589021)
XLA Ops:
  0.0 14.2 %bands.2 = f32[16,264,128]{2,1,0:T(8,128)} custom-call(s32[32]{0:T(128)} %pair_ref.3, bf16[32,64,2049]{2,1,0:T(8,128)(2,1)} %coeffs_ref.3, bf16[2049,32,256]{2,1,0:T(8,128)(2,1)} %bitcast.7, s32[1,32]{1,0:T(1,128)} %bitcast.12), custom_call_target="tpu_custom_call" | custom-call | flops 2148532224 | bytes 10490880 | tf_op jit(solution)/shard_map/bands/pallas_call | solution.py:109
  14.2 6.5 %all-to-all-start = ((f32[16,264,128]{2,1,0:T(8,128)}), f32[16,264,128]{2,1,0:T(8,128)S(1)}, u32[]{:S(2)}, u32[]{:S(2)}) async-start(f32[16,264,128]{2,1,0:T(8,128)} %bands.2), calls=%async_computation | async-start | bytes 4325376 | tf_op jit(solution)/shard_map/all_to_all | solution.py:204
  20.7 30.5 %bands.3 = f32[16,4,192,128]{3,2,1,0:T(8,128)} custom-call(s32[32]{0:T(128)} %pair_ref.3, bf16[32,64,2049]{2,1,0:T(8,128)(2,1)} %coeffs_ref.3, bf16[2049,32,256]{2,1,0:T(8,128)(2,1)} %bitcast.8), custom_call_target="tpu_custom_call" | custom-call | flops 6445596672 | bytes 31472640 | tf_op jit(solution)/shard_map/bands/pallas_call | solution.py:109
  51.2 18.3 %all-to-all-done.refs_0_ = f32[16,264,128]{2,1,0:T(8,128)S(1)} async-done(((f32[16,264,128]{2,1,0:T(8,128)}), f32[16,264,128]{2,1,0:T(8,128)S(1)}, u32[]{:S(2)}, u32[]{:S(2)}) %all-to-all-start) | async-done | bytes 2162720 | tf_op jit(solution)/shard_map/all_to_all | solution.py:204
  69.5 4.8 %all-to-all-start.1 = ((f32[16,768,128]{2,1,0:T(8,128)}), f32[16,768,128]{2,1,0:T(8,128)}, u32[]{:S(2)}, u32[]{:S(2)}) async-start(f32[16,768,128]{2,1,0:T(8,128)} %bitcast.9), calls=%async_computation.1 | async-start | bytes 12582912 | tf_op jit(solution)/shard_map/all_to_all | solution.py:204
  74.3 0.1 slice.14
  74.4 0.1 reshape.43
  74.5 0.1 reshape.44
  74.6 0.2 fusion
  74.9 136.8 %all-to-all-done.1 = f32[16,768,128]{2,1,0:T(8,128)} async-done(((f32[16,768,128]{2,1,0:T(8,128)}), f32[16,768,128]{2,1,0:T(8,128)}, u32[]{:S(2)}, u32[]{:S(2)}) %all-to-all-start.1) | async-done | bytes 6291488 | tf_op jit(solution)/shard_map/all_to_all | solution.py:204
  211.7 10.3 %place.1 = f32[32,64,1024]{2,1,0:T(8,128)} custom-call(s32[1]{0:T(128)} %bitcast.south_ref, bf16[512,512]{1,0:T(8,128)(2,1)S(1)} %get-tuple-element.5.low_ref, bf16[512,512]{1,0:T(8,128)(2,1)S(1)} %get-tuple-element.6.high_ref, f32[16,264,128]{2,1,0:T(8,128)S(1)} %all-to-all-done.refs_0_, f32[16,4,192,128]{3,2,1,0:T(8,128)} %bitcast.5.refs_1_), custom_call_target="tpu_custom_call" | custom-call | tf_op jit(solution)/shard_map/place/pallas_call | solution.py:178
  (5 shorter events, 0.0 us)
Async XLA Ops:
  14.2 55.4 %all-to-all-start = ((f32[16,264,128]{2,1,0:T(8,128)}), f32[16,264,128]{2,1,0:T(8,128)S(1)}, u32[]{:S(2)}, u32[]{:S(2)}) async-start(f32[16,264,128]{2,1,0:T(8,128)} %bands.2), calls=%async_computation | async-start | bytes 4325376 | tf_op jit(solution)/shard_map/all_to_all | solution.py:204
  69.5 142.2 %all-to-all-start.1 = ((f32[16,768,128]{2,1,0:T(8,128)}), f32[16,768,128]{2,1,0:T(8,128)}, u32[]{:S(2)}, u32[]{:S(2)}) async-start(f32[16,768,128]{2,1,0:T(8,128)} %bitcast.9), calls=%async_computation.1 | async-start | bytes 12582912 | tf_op jit(solution)/shard_map/all_to_all | solution.py:204

commit v3 on v2

--- a/solution.py
+++ b/solution.py
@@ -130,8 +130,8 @@
     )(*operands)
 
 
-def place_kernel(south_ref, low_ref, high_ref, *refs):
-    *received, out_ref = refs
+def place_kernel(count, south_ref, low_ref, high_ref, *refs):
+    received, out_ref = refs[:count], refs[-1]
     rows, columns, total = out_ref.shape
     half = total // 2
     south = south_ref[0]
@@ -158,35 +158,44 @@
             out_ref[target, :, start : start + half] = placed[row * columns : (row + 1) * columns]
 
 
-def place(received, pair_ids, south, lats, columns):
+def orders(pair_ids):
     pairs = pair_ids.shape[0]
     column = lax.broadcasted_iota(jnp.int32, (pairs, pairs), 1)
     low = (pair_ids[:, None] == column).astype(jnp.bfloat16)
     high = (pairs - 1 - pair_ids[:, None] == column).astype(jnp.bfloat16)
+    return low, high
+
+
+def place(received, firsts, low, high, south, lats, columns, begin, end, out=None):
+    pairs = low.shape[0]
     steps = lats // TILE
 
     def out_map(i, south_ref):
-        return (jnp.where(south_ref[0] == 1, steps - 1 - i, i), 0, 0)
+        return (jnp.where(south_ref[0] == 1, steps - 1 - begin - i, begin + i), 0, 0)
 
     whole = pl.BlockSpec((pairs, pairs), lambda i, s: (0, 0))
     pieces = [
-        pl.BlockSpec((piece.shape[0], TILE * TILE, piece.shape[2]), lambda i, s: (0, i, 0))
+        pl.BlockSpec((piece.shape[0], TILE * TILE, piece.shape[2]), lambda i, s, at=begin - first: (0, i + at, 0))
         if len(piece.shape) == 3
-        else pl.BlockSpec((piece.shape[0], 1) + piece.shape[2:], lambda i, s: (0, i, 0, 0))
-        for piece in received
+        else pl.BlockSpec(
+            (piece.shape[0], 1) + piece.shape[2:], lambda i, s, at=begin - first: (0, i + at, 0, 0)
+        )
+        for piece, first in zip(received, firsts)
     ]
+    before = [] if out is None else [out]
     return pl.pallas_call(
-        place_kernel,
+        functools.partial(place_kernel, len(received)),
         grid_spec=pltpu.PrefetchScalarGridSpec(
             num_scalar_prefetch=1,
-            grid=(steps,),
-            in_specs=[whole, whole] + pieces,
+            grid=(end - begin,),
+            in_specs=[whole, whole] + pieces + [pl.BlockSpec(memory_space=pl.ANY) for _ in before],
             out_specs=pl.BlockSpec((TILE, columns, 2 * pairs), out_map),
         ),
         out_shape=jax.ShapeDtypeStruct((lats, columns, 2 * pairs), jnp.float32),
         compiler_params=pltpu.CompilerParams(vmem_limit_bytes=48 * 1024 * 1024),
+        input_output_aliases={3 + len(received): 0} if before else {},
         name="place",
-    )(south, low, high, *received)
+    )(south, low, high, *received, *before)
 
 
 def shards(coeffs, legendre, assign):
@@ -196,17 +205,27 @@
     lats = 2 * legendre.shape[1] // devices
     turned = jnp.transpose(legendre, (2, 0, 1))
     tiles = slots // TILE
-    received = []
-    for chunk, steps in ((0, 1), (1, tiles - 1)):
-        if steps:
-            sent = bands(coeffs, turned, assign, chunk, steps, devices)
-            flat = sent.reshape(devices, -1, 2 * columns)
-            piece = lax.all_to_all(flat, "ma", 0, 0, tiled=True)
-            received.append(piece.reshape(sent.shape))
-    all_pairs = received[0][:, TILE * lats, :slots].astype(jnp.int32)
-    order = [all_pairs[:, :TILE].reshape(-1), all_pairs[:, TILE:].reshape(-1)]
+    groups = lats // TILE
+
+    def exchange(sent):
+        flat = sent.reshape(devices, -1, 2 * columns)
+        return lax.all_to_all(flat, "ma", 0, 0, tiled=True).reshape(sent.shape)
+
+    lead = exchange(bands(coeffs, turned, assign, 0, 1, devices))
+    all_pairs = lead[:, TILE * lats, :slots].astype(jnp.int32)
+    low, high = orders(jnp.concatenate([all_pairs[:, :TILE].reshape(-1), all_pairs[:, TILE:].reshape(-1)]))
     south = (me >= devices // 2).astype(jnp.int32).reshape(1)
-    return place(received, jnp.concatenate(order), south, lats, columns)
+    if tiles == 1:
+        return place([lead], [0], low, high, south, lats, columns, 0, groups)
+    sent = bands(coeffs, turned, assign, 1, tiles - 1, devices)
+    cut = max(groups - 1, 0)
+    out, pieces = None, []
+    for begin, end in ((0, cut), (cut, groups)):
+        if end > begin:
+            pieces.append((begin, end, exchange(sent[:, begin:end])))
+    for begin, end, piece in pieces:
+        out = place([lead, piece], [0, begin], low, high, south, lats, columns, begin, end, out)
+    return out
 
 
 def solution(mesh):

time: 222 us -> 224 us (level)
  waiting for transfers between devices: 155 us -> 142 us
  local copies, waits for them, and re-layouts: 0.28 us -> 8.05 us
  starting transfers between devices: 11.3 us -> 16.1 us
  Pallas kernels: 55 us -> 57.6 us
    all_to_all x2 -> x3, waiting for transfers between devices: 155 us -> 142 us  [exchange(): return lax.all_to_all(flat, 'ma', 0, 0, tiled=True).reshape(sent.shape)]
    slice x1 -> x2, local copies, waits for them, and re-layouts: 0.07 us -> 5.11 us  [the longest x1 5.04 us: shards(): pieces.append((begin, end, exchange(sent[:, begin:end])))]
    all_to_all x2 -> x3, starting transfers between devices: 11.3 us -> 16.1 us  [exchange(): return lax.all_to_all(flat, 'ma', 0, 0, tiled=True).reshape(sent.shape)]
    reshape x2 -> x3, local copies, waits for them, and re-layouts: 0.17 us -> 2.9 us  [the longest x1 2.73 us: exchange(): flat = sent.reshape(devices, -1, 2 * columns)]
    pallas_call x1 -> x2, Pallas kernels: 10.3 us -> 12.9 us  [place(): pl.pallas_call(functools.partial(place_kernel, len(received)), grid_spec=...]
  transfers between devices with their start and end apart: 2 -> 3, of which waited for: 2 -> 3; matrix products, arithmetic and copies ran while one was open for 0% -> 4% of each run, Pallas kernels for 14% -> 17%
where the time goes in v3:
time: 224 us
  waiting for transfers between devices  142 us (63%)
  Pallas kernels  57.6 us (26%)
  starting transfers between devices  16.1 us (7%)
  local copies, waits for them, and re-layouts  8.05 us (4%)
    all_to_all x3, waiting for transfers between devices, exchange(): return lax.all_to_all(flat, 'ma', 0, 0, tiled=True).reshape(sent.shape)  142 us
    pallas_call x2, Pallas kernels, bands(): pl.pallas_call(functools.partial(bands_kernel, chunk, extra), grid_spec=p...  44.7 us
    all_to_all x3, starting transfers between devices, exchange(): return lax.all_to_all(flat, 'ma', 0, 0, tiled=True).reshape(sent.shape)  16.1 us
    pallas_call x2, Pallas kernels, place(): pl.pallas_call(functools.partial(place_kernel, len(received)), grid_spec=...  12.9 us
    slice x1, local copies, waits for them, and re-layouts, shards(): pieces.append((begin, end, exchange(sent[:, begin:end])))  5.04 us
  transfers between devices with their start and end apart: 3, of which 3 were waited for; matrix products, arithmetic and copies ran while one was open for 4% of the time, Pallas kernels for 17%

profile of v3, /device:TPU:11, one launch (start us, length us, event | category | flops | bytes accessed | tf_op | source)
XLA Modules:
  0.0 223.6 jit_solution(5593545467342384442)
XLA Ops:
  0.0 14.2 %bands.2 = f32[16,264,128]{2,1,0:T(8,128)} custom-call(s32[32]{0:T(128)} %pair_ref.3, bf16[32,64,2049]{2,1,0:T(8,128)(2,1)} %coeffs_ref.3, bf16[2049,32,256]{2,1,0:T(8,128)(2,1)} %bitcast.12, s32[1,32]{1,0:T(1,128)} %bitcast.17), custom_call_target="tpu_custom_call" | custom-call | flops 2148532224 | bytes 10490880 | tf_op jit(solution)/shard_map/bands/pallas_call | solution.py:109
  14.2 6.5 %all-to-all-start = ((f32[16,264,128]{2,1,0:T(8,128)}), f32[16,264,128]{2,1,0:T(8,128)S(1)}, u32[]{:S(2)}, u32[]{:S(2)}) async-start(f32[16,264,128]{2,1,0:T(8,128)} %bands.2), calls=%async_computation | async-start | bytes 4325376 | tf_op jit(solution)/shard_map/all_to_all | solution.py:212
  20.7 30.5 %bands.3 = f32[16,4,192,128]{3,2,1,0:T(8,128)} custom-call(s32[32]{0:T(128)} %pair_ref.3, bf16[32,64,2049]{2,1,0:T(8,128)(2,1)} %coeffs_ref.3, bf16[2049,32,256]{2,1,0:T(8,128)(2,1)} %bitcast.13), custom_call_target="tpu_custom_call" | custom-call | flops 6445596672 | bytes 31472640 | tf_op jit(solution)/shard_map/bands/pallas_call | solution.py:109
  51.2 5.0 %slice.24 = f32[16,3,192,128]{3,2,1,0:T(8,128)} slice(f32[16,4,192,128]{3,2,1,0:T(8,128)} %bands.3), slice={[0:16], [0:3], [0:192], [0:128]} | slice | bytes 9437184 | tf_op jit(solution)/shard_map/slice | solution.py:225
  56.2 13.3 %all-to-all-done.refs_0_ = f32[16,264,128]{2,1,0:T(8,128)S(1)} async-done(((f32[16,264,128]{2,1,0:T(8,128)}), f32[16,264,128]{2,1,0:T(8,128)S(1)}, u32[]{:S(2)}, u32[]{:S(2)}) %all-to-all-start) | async-done | bytes 2162720 | tf_op jit(solution)/shard_map/all_to_all | solution.py:212
  69.5 4.8 %all-to-all-start.2 = ((f32[16,576,128]{2,1,0:T(8,128)}), f32[16,576,128]{2,1,0:T(8,128)}, u32[]{:S(2)}, u32[]{:S(2)}) async-start(f32[16,576,128]{2,1,0:T(8,128)} %bitcast.14), calls=%async_computation.2 | async-start | bytes 9437184 | tf_op jit(solution)/shard_map/all_to_all | solution.py:212
  74.3 2.7 %slice_bitcast_fusion = f32[16,192,128]{2,1,0:T(8,128)} fusion(f32[16,4,192,128]{3,2,1,0:T(8,128)} %bands.3), kind=kLoop, calls=%fused_computation | loop fusion | bytes 3145728 | tf_op jit(solution)/shard_map/reshape | solution.py:211
  77.0 101.0 %all-to-all-done.2 = f32[16,576,128]{2,1,0:T(8,128)} async-done(((f32[16,576,128]{2,1,0:T(8,128)}), f32[16,576,128]{2,1,0:T(8,128)}, u32[]{:S(2)}, u32[]{:S(2)}) %all-to-all-start.2) | async-done | bytes 4718624 | tf_op jit(solution)/shard_map/all_to_all | solution.py:212
  178.0 4.8 %all-to-all-start.1 = ((f32[16,192,128]{2,1,0:T(8,128)}), f32[16,192,128]{2,1,0:T(8,128)}, u32[]{:S(2)}, u32[]{:S(2)}) async-start(f32[16,192,128]{2,1,0:T(8,128)} %slice_bitcast_fusion), calls=%async_computation.1 | async-start | bytes 3145728 | tf_op jit(solution)/shard_map/all_to_all | solution.py:212
  182.8 0.1 slice.22
  182.9 0.1 reshape.49
  183.0 0.1 reshape.50
  183.1 0.2 fusion
  183.4 8.5 %place.2.refs_2_ = f32[32,64,1024]{2,1,0:T(8,128)} custom-call(s32[1]{0:T(128)} %bitcast.south_ref, bf16[512,512]{1,0:T(8,128)(2,1)S(1)} %get-tuple-element.5.low_ref, bf16[512,512]{1,0:T(8,128)(2,1)S(1)} %get-tuple-element.6.high_ref, f32[16,264,128]{2,1,0:T(8,128)S(1)} %all-to-all-done.refs_0_, f32[16,3,192,128]{3,2,1,0:T(8,128)} %bitcast.7.refs_1_), custom_call_target="tpu_custom_call" | custom-call | tf_op jit(solution)/shard_map/place/pallas_call | solution.py:186
  191.8 27.3 %all-to-all-done.1 = f32[16,192,128]{2,1,0:T(8,128)} async-done(((f32[16,192,128]{2,1,0:T(8,128)}), f32[16,192,128]{2,1,0:T(8,128)}, u32[]{:S(2)}, u32[]{:S(2)}) %all-to-all-start.1) | async-done | bytes 1572896 | tf_op jit(solution)/shard_map/all_to_all | solution.py:212
  219.1 4.5 %place.3 = f32[32,64,1024]{2,1,0:T(8,128)} custom-call(s32[1]{0:T(128)} %bitcast.south_ref, bf16[512,512]{1,0:T(8,128)(2,1)S(1)} %get-tuple-element.5.low_ref, bf16[512,512]{1,0:T(8,128)(2,1)S(1)} %get-tuple-element.6.high_ref, f32[16,264,128]{2,1,0:T(8,128)S(1)} %all-to-all-done.refs_0_, ...), custom_call_target="tpu_custom_call", output_to_operand_aliasing={{}: (5, {})} | custom-call | tf_op jit(solution)/shard_map/place/pallas_call | solution.py:186
  (5 shorter events, 0.0 us)
Async XLA Ops:
  14.2 55.4 %all-to-all-start = ((f32[16,264,128]{2,1,0:T(8,128)}), f32[16,264,128]{2,1,0:T(8,128)S(1)}, u32[]{:S(2)}, u32[]{:S(2)}) async-start(f32[16,264,128]{2,1,0:T(8,128)} %bands.2), calls=%async_computation | async-start | bytes 4325376 | tf_op jit(solution)/shard_map/all_to_all | solution.py:212
  69.5 108.5 %all-to-all-start.2 = ((f32[16,576,128]{2,1,0:T(8,128)}), f32[16,576,128]{2,1,0:T(8,128)}, u32[]{:S(2)}, u32[]{:S(2)}) async-start(f32[16,576,128]{2,1,0:T(8,128)} %bitcast.14), calls=%async_computation.2 | async-start | bytes 9437184 | tf_op jit(solution)/shard_map/all_to_all | solution.py:212
  178.0 41.1 %all-to-all-start.1 = ((f32[16,192,128]{2,1,0:T(8,128)}), f32[16,192,128]{2,1,0:T(8,128)}, u32[]{:S(2)}, u32[]{:S(2)}) async-start(f32[16,192,128]{2,1,0:T(8,128)} %slice_bitcast_fusion), calls=%async_computation.1 | async-start | bytes 3145728 | tf_op jit(solution)/shard_map/all_to_all | solution.py:212
